TPU v7x, 256 devices: a whole 4x4x8 slice. The times are simulated.
256 devices in a mesh: robot: 64 (over x, z, core), sub: 4 (over y).
Axes of the slice: x: 4, y: 4, z: 8, core: 2. Of those that a mesh axis runs over, the one named last changes fastest.
Arguments:
- landmark_copies: float32 [64, 4, 3, 4096], P('robot', 'sub'), may hold values from -6 to 6
- dual_copies: float32 [64, 4, 3, 4096], P('robot', 'sub'), may hold values from -4 to 4
- visibility: int32 [64, 4, 4096], P('robot', 'sub'), may hold values from 0 to 511
- block_counts: int32 [64, 4, 64], P('robot', 'sub'), may hold values from 1 to 64, as said below
- consensus_old: float32 [64, 4, 3, 512], P('robot', 'sub'), may hold values from -6 to 6
- poses: float32 [64, 4, 6, 1024], P('robot', 'sub'), may hold values from -6 to 6
- inverse_blocks: float32 [64, 4, 36, 1024], P('robot', 'sub'), may hold values from -1.8 to 1.8
- jacobians: float32 [64, 4, 18, 4096], P('robot', 'sub'), may hold values from -3 to 3
- measurements: float32 [64, 4, 3, 4096], P('robot', 'sub'), may hold values from -6 to 6
- obs_pose: int32 [64, 4, 4096], P('robot', 'sub'), may hold values from 0 to 1023
- obs_slot: int32 [64, 4, 4096], P('robot', 'sub'), may hold values from 0 to 4095, as said below
- edge_to: int32 [64, 4, 1024], P('robot', 'sub'), may hold values from 0 to 4095
- edge_offset: float32 [64, 4, 6, 1024], P('robot', 'sub'), may hold values from -3 to 3
Outputs:
- refined_poses: float32 [64, 4, 6, 1024], P('robot', 'sub')
- consensus: float32 [64, 4, 3, 512], P('robot', 'sub')
- dual_new: float32 [64, 4, 3, 4096], P('robot', 'sub')
- residual_norms: float32 [2], replicated
Inputs may be any that keep to these rules, and one draw needn't show every extreme that they name: block_counts[r,s,d] counts the live slots at the head of block d; for every sub index some robot receives full blocks from every robot, which robot varies with the draw. `obs_slot`: each observation names a live slot of its own device.
All inputs are finite; a program needn't handle non-finite values.
Results may differ from a plain program's by a relative error of at most 0.0001.
Values sent between devices are 32-bit elements; how exact they have to be, the bound alone decides.
A program may use at most 64 MiB of HBM per device.

v0:
```python
import jax
import jax.numpy as jnp
from jax import lax
from jax.sharding import Mesh
from jax.sharding import PartitionSpec as P

ROBOT = ("robot_0", "robot_1", "robot_2")
ROBOT_SUB = ("robot_0", "robot_1", "robot_2", "sub")
penalty = 2.0


def over_axes(x, axes):
    for axis in axes:
        x = lax.psum(x, axis)
    return x


def copy_for_each(x, axis):
    length = lax.axis_size(axis)
    return lax.all_to_all(jnp.broadcast_to(x[None], (length, *x.shape)), axis, 0, 0, tiled=True)


def laid_out(pieces, dim):
    dims = list(pieces.shape[1:])
    dims[dim] *= pieces.shape[0]
    return jnp.moveaxis(pieces, 0, dim).reshape(dims)


def collect(x, axis, dim):
    pieces = copy_for_each(x, axis)
    return laid_out(pieces, dim)


def body(
    landmark_copies,
    dual_copies,
    visibility,
    block_counts,
    consensus_old,
    poses,
    inverse_blocks,
    jacobians,
    measurements,
    obs_pose,
    obs_slot,
    edge_to,
    edge_offset,
):
    copies = landmark_copies[0, 0]
    duals = dual_copies[0, 0]
    slot_ids = visibility[0]
    counts = block_counts[0, 0]
    old_estimate = consensus_old[0, 0]
    robots = lax.axis_size(ROBOT)
    slot_count = copies.shape[1]
    block_size = slot_count // robots
    owned = old_estimate.shape[1]
    live_mask = (
        (jnp.arange(block_size)[None, :] < counts[:, None]).reshape(slot_count).astype(jnp.float32)
    )
    outgoing = jnp.concatenate([(copies + duals) * live_mask[None, :], live_mask[None, :]], axis=0)
    received, received_ids = (
        lax.all_to_all(outgoing, ROBOT, split_axis=1, concat_axis=1, tiled=True),
        lax.all_to_all(slot_ids, ROBOT, split_axis=1, concat_axis=1, tiled=True),
    )
    owner_ids = received_ids[0]
    totals = jax.vmap(lambda entries: jax.ops.segment_sum(entries, owner_ids, num_segments=owned))(
        received
    )
    consensus = (old_estimate + totals[:3]) / (1.0 + totals[3:4])
    returning = consensus[:, owner_ids]
    back = lax.all_to_all(returning, ROBOT, split_axis=1, concat_axis=1, tiled=True)
    differ = (copies - back) * live_mask[None, :]
    dual_new = duals + differ
    primal = jnp.sum(differ * differ)
    change = consensus - old_estimate
    dualsum = penalty * penalty * jnp.sum(totals[3:4] * change * change)
    primal_all, dual_all = (over_axes(primal, ROBOT_SUB), over_axes(dualsum, ROBOT_SUB))
    landmark_total = owned * robots * lax.axis_size("sub")
    residual_norms = jnp.sqrt(jnp.stack([primal_all, dual_all]) / landmark_total)
    pose_block = poses[0, 0]
    pose_count = pose_block.shape[1]
    robot_all = collect(pose_block, "sub", 1)
    pose_far = robot_all[:, edge_to[0, 0]]
    copies_at = copies[:, obs_slot[0, 0]]
    error = measurements[0, 0] - copies_at
    jac_rows = jacobians[0, 0].reshape(3, 6, error.shape[1])
    pull = jnp.sum(jac_rows * error[:, None, :], axis=0)
    pose_ids = obs_pose[0, 0]
    grad_obs = jax.vmap(
        lambda entries: jax.ops.segment_sum(entries, pose_ids, num_segments=pose_count)
    )(pull)
    grad = grad_obs + pose_far - pose_block - edge_offset[0, 0]
    inverse = inverse_blocks[0, 0].reshape(6, 6, pose_count)
    delta = jnp.sum(inverse * grad[None, :, :], axis=1)
    refined = pose_block + delta
    return (refined[None, None], consensus[None, None], dual_new[None, None], residual_norms)


def solution(mesh):
    finer = Mesh(
        mesh.devices.reshape(4, 8, 2, mesh.shape["sub"]), ("robot_0", "robot_1", "robot_2", "sub")
    )
    return jax.shard_map(
        body,
        mesh=finer,
        in_specs=(
            P(ROBOT, "sub", None, None),
            P(ROBOT, "sub", None, None),
            P(ROBOT, "sub", None),
            P(ROBOT, "sub", None),
            P(ROBOT, "sub", None, None),
            P(ROBOT, "sub", None, None),
            P(ROBOT, "sub", None, None),
            P(ROBOT, "sub", None, None),
            P(ROBOT, "sub", None, None),
            P(ROBOT, "sub", None),
            P(ROBOT, "sub", None),
            P(ROBOT, "sub", None),
            P(ROBOT, "sub", None, None),
        ),
        out_specs=(
            P(ROBOT, "sub", None, None),
            P(ROBOT, "sub", None, None),
            P(ROBOT, "sub", None, None),
            P(),
        ),
        check_vma=False,
    )
```

profile of v0, /device:TPU:2, one launch (start us, length us, event | category | flops | bytes accessed | tf_op | source)
XLA Modules:
  0.0 214.0 jit_solution(6350417667022919930)
XLA Ops:
  0.7 0.5 broadcast.121
  1.2 1.4 reduce.16
  2.6 0.7 all_to_all.26
  3.3 12.0 %all-to-all-start.1 = ((s32[1,64,64]{2,0,1:T(1,128)}), s32[1,64,64]{2,0,1:T(1,128)S(1)}, u32[]{:S(2)}, u32[]{:S(2)}) async-start(s32[1,64,64]{2,0,1:T(1,128)} %all_to_all.26), calls=%async_computation.1 | async-start | bytes 65536 | tf_op jit(solution)/shard_map/all_to_all | solution.py:64
  15.3 0.7 fusion.8
  16.1 0.7 fusion.9
  16.8 1.4 copy.54
  18.2 0.2 add_reduce_fusion.1
  18.4 0.1 add.91
  18.6 2.0 copy.53
  20.6 14.1 %gather_fusion.1 = f32[4096,3]{1,0:T(8,128)} fusion(f32[3,4096]{0,1:T(8,128)S(1)} %bitcast.57, s32[4096]{0:T(1024)S(1)} %broadcast_clamp_fusion.1), kind=kCustom, calls=%fused_computation.1 | custom fusion | bytes 114688 | tf_op jit(solution)/shard_map/gather | solution.py:85
  34.6 3.7 %bitcast_subtract_fusion.1 = f32[3,4096]{0,1:T(8,128)} fusion(f32[4096,3]{1,0:T(8,128)} %gather_fusion.1, f32[1,1,3,4096]{2,3,1,0:T(8,128)} %copy.53), kind=kLoop, calls=%fused_computation.9 | loop fusion | flops 12288 | bytes 147456 | tf_op jit(solution)/shard_map/sub | solution.py:86
  38.4 2.3 %copy.55 = f32[3,4096]{1,0:T(4,128)S(1)} copy(f32[3,4096]{0,1:T(8,128)} %bitcast_subtract_fusion.1) | data formatting | bytes 98304 | tf_op jit(solution)/shard_map/sub | solution.py:86
  40.6 0.7 reduce.1
  41.6 0.7 reshape.197
  42.2 0.2 copy.50
  42.5 0.1 copy.82
  42.6 0.8 reshape.266
  43.3 0.8 copy.59
  44.2 2.0 copy.56
  46.2 1.0 copy.57
  47.2 1.3 reduce
  48.4 0.7 reshape_squeeze.6
  49.1 0.7 broadcast_in_dim.9
  49.8 4.5 %all-to-all-start = ((f32[4,6,1024]{2,1,0:T(8,128)}), f32[4,6,1024]{2,1,0:T(8,128)S(1)}, u32[]{:S(2)}, u32[]{:S(2)}) async-start(f32[4,6,1024]{2,1,0:T(8,128)} %broadcast_in_dim.9), calls=%async_computation | async-start | bytes 262144 | tf_op jit(solution)/shard_map/all_to_all | solution.py:20
  54.3 0.1 broadcast_in_dim_squeeze.9
  54.4 0.6 broadcast_clamp_fusion
  55.0 0.7 reduce.17
  55.7 0.7 reshape.232
  56.4 3.8 %all-to-all-done = f32[4,6,1024]{2,1,0:T(8,128)S(1)} async-done(((f32[4,6,1024]{2,1,0:T(8,128)}), f32[4,6,1024]{2,1,0:T(8,128)S(1)}, u32[]{:S(2)}, u32[]{:S(2)}) %all-to-all-start) | async-done | bytes 98336 | tf_op jit(solution)/shard_map/all_to_all | solution.py:20
  60.2 10.3 %all-to-all-start.2 = ((f32[64,1,256]{2,1,0:T(1,128)}), f32[64,1,256]{2,1,0:T(1,128)S(1)}, u32[]{:S(2)}, u32[]{:S(2)}) async-start(f32[64,1,256]{2,1,0:T(1,128)} %reshape.266), calls=%async_computation.2 | async-start | bytes 131072 | tf_op jit(solution)/shard_map/all_to_all | solution.py:63
  70.6 1.9 copy.52
  72.5 4.4 %gather_fusion = f32[1024,6]{1,0:T(8,128)S(1)} fusion(f32[6,4096]{0,1:T(8,128)} %bitcast.60, s32[1024]{0:T(1024)S(1)} %broadcast_clamp_fusion.2), kind=kCustom, calls=%fused_computation | custom fusion | bytes 53248 | tf_op jit(solution)/shard_map/gather | solution.py:84
  76.9 22.9 %scatter_fusion = f32[6,1024]{0,1:T(8,128)S(1)} fusion(f32[6,1024]{0,1:T(8,128)S(1)} %bitcast.58, s32[4096]{0:T(1024)} %bitcast.74, f32[4096,6]{1,0:T(8,128)} %copy.56), kind=kCustom, calls=%fused_computation.3 | custom fusion | flops 24576 | bytes 311296 | tf_op jit(solution)/shard_map/vmap()/scatter-add | solution.py:91
  99.8 1.9 bitcast_subtract_fusion.2
  101.7 1.2 copy.58
  102.9 1.0 multiply_reduce_fusion.1
  103.9 0.5 broadcast.123
  104.5 0.8 reduce.18
  105.3 0.1 reshape.267
  105.4 0.1 reshape.231
  105.5 2.0 copy.62
  107.5 22.9 %scatter_custom_fusion.1 = f32[4,512]{0,1:T(8,128)S(1)} fusion(s32[4096]{0:T(1024)} %reshape.232, f32[4096,4]{1,0:T(8,128)} %copy.62, f32[]{:T(128)} %constant.9.clone.1), kind=kCustom, calls=%fused_computation.22 | custom fusion | flops 16384 | bytes 8704 | tf_op jit(solution)/shard_map/vmap()/scatter-add | solution.py:67
  130.4 0.3 slice_reduce_fusion
  130.7 0.8 fusion.3
  131.6 14.1 %gather_fusion.2 = f32[4096,3]{1,0:T(8,128)} fusion(f32[3,512]{0,1:T(8,128)S(1)} %get-tuple-element.31, s32[4096]{0:T(1024)S(1)} %copy-done.6), kind=kCustom, calls=%fused_computation.2 | custom fusion | bytes 114688 | tf_op jit(solution)/shard_map/gather | solution.py:71
  145.6 2.3 %copy.63 = f32[3,64,64]{2,0,1:T(4,128)S(1)} copy(f32[3,64,64]{0,2,1:T(8,128)} %bitcast.61) | data formatting | bytes 98304 | tf_op jit(solution)/shard_map/all_to_all | solution.py:72
  147.9 0.8 reshape.268
  148.7 10.3 %all-to-all-start.3 = ((f32[64,1,192]{2,1,0:T(1,128)}), f32[64,1,192]{2,1,0:T(1,128)S(1)}, u32[]{:S(2)}, u32[]{:S(2)}) async-start(f32[64,1,192]{2,1,0:T(1,128)} %reshape.268), calls=%async_computation.3 | async-start | bytes 131072 | tf_op jit(solution)/shard_map/all_to_all | solution.py:72
  159.0 0.6 reshape_add_fusion
  159.6 0.7 copy.68
  161.0 6.8 %all-to-all-done.3 = f32[64,1,192]{2,1,0:T(1,128)S(1)} async-done(((f32[64,1,192]{2,1,0:T(1,128)}), f32[64,1,192]{2,1,0:T(1,128)S(1)}, u32[]{:S(2)}, u32[]{:S(2)}) %all-to-all-start.3) | async-done | bytes 49184 | tf_op jit(solution)/shard_map/all_to_all | solution.py:72
  167.8 0.8 reduce.19
  168.6 0.1 reshape.269
  168.7 2.0 copy.67
  170.8 0.1 all_to_all.32
  170.9 2.5 %fusion.2 = f32[]{:T(128)} fusion(f32[3,64,64]{0,2,1:T(8,128)} %copy.67, f32[4096]{0:T(1024)S(1)} %copy-done.5, f32[1,1,3,4096]{2,3,1,0:T(8,128)S(1)} %copy.54), kind=kLoop, calls=%fused_computation.8 | loop fusion | flops 49151 | bytes 114692 | tf_op jit(solution)/shard_map/reduce_sum | solution.py:75
  173.4 0.1 copy_add_fusion
  173.5 0.7 copy.69
  174.2 9.8 %all-reduce.2 = (f32[]{:T(128)}, f32[]{:T(128)}) all-reduce(f32[]{:T(128)S(6)} %mul_shard_map.3, f32[]{:T(128)} %fusion.2), channel_id=1, replica_groups=mesh['robot_0'=4,'robot_1'=8,'robot_2'=2,'sub'=4] {'robot_0'}, use_global_device_ids=true, to_apply=%region_10.0 | all-reduce | flops 2 | bytes 16 | tf_op jit(solution)/shard_map/psum | solution.py:14
  184.0 15.5 %all-reduce = (f32[]{:T(128)}, f32[]{:T(128)}) all-reduce(f32[]{:T(128)} %get-tuple-element.26, f32[]{:T(128)} %get-tuple-element.27), channel_id=1, replica_groups=mesh['robot_0'=4,'robot_1'=8,'robot_2'=2,'sub'=4] {'robot_1'}, use_global_device_ids=true, to_apply=%region_11.0 | all-reduce | flops 2 | bytes 16 | tf_op jit(solution)/shard_map/psum | solution.py:14
  199.5 3.2 %all-reduce.3 = (f32[]{:T(128)}, f32[]{:T(128)}) all-reduce(f32[]{:T(128)} %get-tuple-element.22, f32[]{:T(128)} %get-tuple-element.23), channel_id=1, replica_groups=mesh['robot_0'=4,'robot_1'=8,'robot_2'=2,'sub'=4] {'robot_2'}, use_global_device_ids=true, to_apply=%region_12.0 | all-reduce | flops 2 | bytes 16 | tf_op jit(solution)/shard_map/psum | solution.py:14
  202.7 9.5 %all-reduce.1 = (f32[1]{0:T(128)}, f32[1]{0:T(128)}) all-reduce(f32[1]{0:T(128)} %bitcast.24, f32[1]{0:T(128)} %bitcast.23), channel_id=1, replica_groups=mesh['robot_0'=4,'robot_1'=8,'robot_2'=2,'sub'=4] {'sub'}, use_global_device_ids=true, to_apply=%region_13.0 | all-reduce | flops 2 | bytes 16 | tf_op jit(solution)/shard_map/psum | solution.py:14
  212.2 1.8 fusion.10
  (36 shorter events, 0.3 us)
Async XLA Ops:
  0.6 17.6 %copy-start = (f32[1,1,3,4096]{3,1,2,0:T(1,128)S(1)}, f32[1,1,3,4096]{3,1,2,0:T(1,128)}, u32[]{:S(2)}) copy-start(f32[1,1,3,4096]{3,1,2,0:T(1,128)} %param.13) | copy-start | bytes 147460
  0.6 17.6 %copy-start.3 = (f32[1,1,3,4096]{3,1,2,0:T(1,128)S(1)}, f32[1,1,3,4096]{3,1,2,0:T(1,128)}, u32[]{:S(2)}) copy-start(f32[1,1,3,4096]{3,1,2,0:T(1,128)} %param.14) | copy-start | bytes 147460
  0.7 17.9 %copy-start.9 = (s32[1,1,4096]{2,1,0:T(1,128)S(1)}, s32[1,1,4096]{2,1,0:T(1,128)}, u32[]{:S(2)}) copy-start(s32[1,1,4096]{2,1,0:T(1,128)} %param.23) | copy-start | bytes 49156
  0.7 17.9 %copy-start.7 = (f32[1,1,3,4096]{3,1,2,0:T(1,128)S(1)}, f32[1,1,3,4096]{3,1,2,0:T(1,128)}, u32[]{:S(2)}) copy-start(f32[1,1,3,4096]{3,1,2,0:T(1,128)} %param.21) | copy-start | bytes 147460
  3.3 45.8 %all-to-all-start.1 = ((s32[1,64,64]{2,0,1:T(1,128)}), s32[1,64,64]{2,0,1:T(1,128)S(1)}, u32[]{:S(2)}, u32[]{:S(2)}) async-start(s32[1,64,64]{2,0,1:T(1,128)} %all_to_all.26), calls=%async_computation.1 | async-start | bytes 65536 | tf_op jit(solution)/shard_map/all_to_all | solution.py:64
  38.4 2.3 %copy-start.1 = (f32[1,1,18,4096]{3,1,2,0:T(1,128)S(1)}, f32[1,1,18,4096]{3,1,2,0:T(1,128)}, u32[]{:S(2)}) copy-start(f32[1,1,18,4096]{3,1,2,0:T(1,128)} %param.20) | copy-start | bytes 884740
  38.4 3.0 %copy-start.10 = (s32[1,1,1024]{2,1,0:T(1,128)S(1)}, s32[1,1,1024]{2,1,0:T(1,128)}, u32[]{:S(2)}) copy-start(s32[1,1,1024]{2,1,0:T(1,128)} %param.24) | copy-start | bytes 12292
  38.4 3.9 %copy-start.2 = (f32[1,1,6,1024]{3,1,2,0:T(1,128)S(1)}, f32[1,1,6,1024]{3,1,2,0:T(1,128)}, u32[]{:S(2)}) copy-start(f32[1,1,6,1024]{3,1,2,0:T(1,128)} %param.18) | copy-start | bytes 73732
  41.5 4.6 %copy-start.8 = (f32[1,1,6,1024]{3,1,2,0:T(1,128)S(1)}, f32[1,1,6,1024]{3,1,2,0:T(1,128)}, u32[]{:S(2)}) copy-start(f32[1,1,6,1024]{3,1,2,0:T(1,128)} %param.25) | copy-start | bytes 73732
  49.8 10.4 %all-to-all-start = ((f32[4,6,1024]{2,1,0:T(8,128)}), f32[4,6,1024]{2,1,0:T(8,128)S(1)}, u32[]{:S(2)}, u32[]{:S(2)}) async-start(f32[4,6,1024]{2,1,0:T(8,128)} %broadcast_in_dim.9), calls=%async_computation | async-start | bytes 262144 | tf_op jit(solution)/shard_map/all_to_all | solution.py:20
  60.2 43.7 %all-to-all-start.2 = ((f32[64,1,256]{2,1,0:T(1,128)}), f32[64,1,256]{2,1,0:T(1,128)S(1)}, u32[]{:S(2)}, u32[]{:S(2)}) async-start(f32[64,1,256]{2,1,0:T(1,128)} %reshape.266), calls=%async_computation.2 | async-start | bytes 131072 | tf_op jit(solution)/shard_map/all_to_all | solution.py:63
  105.3 26.3 %copy-start.6 = (s32[4096]{0:T(1024)S(1)}, s32[4096]{0:T(1024)}, u32[]{:S(2)}) copy-start(s32[4096]{0:T(1024)} %broadcast_clamp_fusion) | copy-start | bytes 49156
  147.9 23.0 %copy-start.5 = (f32[4096]{0:T(1024)S(1)}, f32[4096]{0:T(1024)}, u32[]{:S(2)}) copy-start(f32[4096]{0:T(1024)} %reshape.197) | copy-start | bytes 49156
  148.7 19.1 %all-to-all-start.3 = ((f32[64,1,192]{2,1,0:T(1,128)}), f32[64,1,192]{2,1,0:T(1,128)S(1)}, u32[]{:S(2)}, u32[]{:S(2)}) async-start(f32[64,1,192]{2,1,0:T(1,128)} %reshape.268), calls=%async_computation.3 | async-start | bytes 131072 | tf_op jit(solution)/shard_map/all_to_all | solution.py:72
  170.9 2.6 %copy-start.4 = (f32[1,1,3,4096]{3,1,2,0:T(1,128)S(1)}, f32[1,1,3,4096]{3,1,2,0:T(1,128)}, u32[]{:S(2)}) copy-start(f32[1,1,3,4096]{3,1,2,0:T(1,128)} %param.14) | copy-start | bytes 147460
where the time goes:
time: 215 us; the launch traced here: 214 us
  other arithmetic  66.6 us (31%)
  local copies, waits for them, and re-layouts  59.9 us (28%)
  blocking collectives  38 us (18%)
  starting transfers between devices  37.1 us (17%)
  waiting for transfers between devices  10.7 us (5%)
    psum x4, blocking collectives, over_axes(): x = lax.psum(x, axis)  38 us
    scatter-add x1, other arithmetic, body(): jax.ops.segment_sum(entries, owner_ids, num_segments=owned)  22.9 us
    scatter-add x1, other arithmetic, body(): jax.ops.segment_sum(entries, pose_ids, num_segments=pose_count)  22.9 us
    gather x1, local copies, waits for them, and re-layouts, body(): copies_at = copies[:, obs_slot[0, 0]]  14.1 us
    gather x1, local copies, waits for them, and re-layouts, body(): returning = consensus[:, owner_ids]  14.1 us
    all_to_all x1, starting transfers between devices, body(): lax.all_to_all(slot_ids, ROBOT, split_axis=1, concat_axis=1, tiled=True)  12 us
    all_to_all x1, starting transfers between devices, body(): lax.all_to_all(returning, ROBOT, split_axis=1, concat_axis=1, tiled=True)  10.3 us
    all_to_all x1, starting transfers between devices, body(): lax.all_to_all(outgoing, ROBOT, split_axis=1, concat_axis=1, tiled=True)  10.3 us
  transfers between devices with their start and end apart: 4, of which 2 were waited for; matrix products, arithmetic and copies ran while one was open for 33% of the time, Pallas kernels for 0%

commit v1 on v0

--- a/solution.py
+++ b/solution.py
@@ -11,7 +11,7 @@
 
 def over_axes(x, axes):
     for axis in axes:
-        x = lax.psum(x, axis)
+        x = jnp.sum(lax.all_gather(x, axis), axis=0)
     return x
 
 

time: 215 us -> 231 us (1.074)
  local copies, waits for them, and re-layouts: 59.9 us -> 74.7 us
  other arithmetic: 66.6 us -> 71.6 us
  blocking collectives: 38 us -> 35.3 us
    psum x4 -> x0, blocking collectives: 38 us -> none  [over_axes(): x = lax.psum(x, axis)]
    unnamed x0 -> x4, blocking collectives: none -> 35.3 us
    unnamed x34 -> x56, local copies, waits for them, and re-layouts: 9.16 us -> 23.9 us
    reduce_sum x0 -> x8, other arithmetic: none -> 4.88 us  [over_axes(): x = jnp.sum(lax.all_gather(x, axis), axis=0)]
where the time goes in v1:
time: 231 us; the launch traced here: 230 us
  local copies, waits for them, and re-layouts  74.7 us (32%)
  other arithmetic  71.6 us (31%)
  starting transfers between devices  37.1 us (16%)
  blocking collectives  35.3 us (15%)
  waiting for transfers between devices  9.95 us (4%)
    unnamed x4, blocking collectives  35.3 us
    unnamed x56, local copies, waits for them, and re-layouts  23.9 us
    scatter-add x1, other arithmetic, body(): jax.ops.segment_sum(entries, owner_ids, num_segments=owned)  22.9 us
    scatter-add x1, other arithmetic, body(): jax.ops.segment_sum(entries, pose_ids, num_segments=pose_count)  22.9 us
    gather x1, local copies, waits for them, and re-layouts, body(): copies_at = copies[:, obs_slot[0, 0]]  14.1 us
    gather x1, local copies, waits for them, and re-layouts, body(): returning = consensus[:, owner_ids]  14.1 us
    all_to_all x1, starting transfers between devices, body(): lax.all_to_all(slot_ids, ROBOT, split_axis=1, concat_axis=1, tiled=True)  12 us
    all_to_all x1, starting transfers between devices, body(): lax.all_to_all(returning, ROBOT, split_axis=1, concat_axis=1, tiled=True)  10.3 us
  transfers between devices with their start and end apart: 4, of which 2 were waited for; matrix products, arithmetic and copies ran while one was open for 33% of the time, Pallas kernels for 0%

profile of v1, /device:TPU:2, one launch (start us, length us, event | category | flops | bytes accessed | tf_op | source)
XLA Modules:
  0.0 230.3 jit_solution(12217671549824149363)
XLA Ops:
  1.2 1.4 reduce.24
  2.6 0.7 all_to_all.26
  3.3 12.0 %all-to-all-start.1 = ((s32[1,64,64]{2,0,1:T(1,128)}), s32[1,64,64]{2,0,1:T(1,128)S(1)}, u32[]{:S(2)}, u32[]{:S(2)}) async-start(s32[1,64,64]{2,0,1:T(1,128)} %all_to_all.26), calls=%async_computation.1 | async-start | bytes 65536 | tf_op jit(solution)/shard_map/all_to_all | solution.py:64
  15.3 0.7 fusion.8
  16.1 0.7 fusion.9
  16.8 1.4 copy.54
  18.6 2.0 copy.53
  20.6 14.1 %gather_fusion.1 = f32[4096,3]{1,0:T(8,128)} fusion(f32[3,4096]{0,1:T(8,128)S(1)} %bitcast.69, s32[4096]{0:T(1024)S(1)} %broadcast_clamp_fusion.1), kind=kCustom, calls=%fused_computation.1 | custom fusion | bytes 114688 | tf_op jit(solution)/shard_map/gather | solution.py:85
  34.6 3.7 %bitcast_subtract_fusion.1 = f32[3,4096]{0,1:T(8,128)} fusion(f32[4096,3]{1,0:T(8,128)} %gather_fusion.1, f32[1,1,3,4096]{2,3,1,0:T(8,128)} %copy.53), kind=kLoop, calls=%fused_computation.9 | loop fusion | flops 12288 | bytes 147456 | tf_op jit(solution)/shard_map/sub | solution.py:86
  38.4 2.3 copy.55
  40.6 0.7 reduce.9
  41.6 0.7 reshape.197
  42.6 0.8 reshape.306
  43.3 0.8 copy.59
  44.2 1.3 dynamic-slice
  45.5 1.3 dynamic-slice.1
  46.7 1.2 dynamic-slice.2
  48.0 0.7 dynamic-slice.3
  48.7 2.0 copy.56
  50.7 1.0 copy.57
  51.7 1.3 reduce.8
  52.9 0.7 reshape_squeeze.6
  53.6 0.7 broadcast_in_dim.9
  54.3 4.5 %all-to-all-start = ((f32[4,6,1024]{2,1,0:T(8,128)}), f32[4,6,1024]{2,1,0:T(8,128)S(1)}, u32[]{:S(2)}, u32[]{:S(2)}) async-start(f32[4,6,1024]{2,1,0:T(8,128)} %broadcast_in_dim.9), calls=%async_computation | async-start | bytes 262144 | tf_op jit(solution)/shard_map/all_to_all | solution.py:20
  58.9 0.6 broadcast_clamp_fusion
  59.5 0.7 reduce.25
  60.2 0.7 reshape.232
  60.9 3.8 %all-to-all-done = f32[4,6,1024]{2,1,0:T(8,128)S(1)} async-done(((f32[4,6,1024]{2,1,0:T(8,128)}), f32[4,6,1024]{2,1,0:T(8,128)S(1)}, u32[]{:S(2)}, u32[]{:S(2)}) %all-to-all-start) | async-done | bytes 98336 | tf_op jit(solution)/shard_map/all_to_all | solution.py:20
  64.7 10.3 %all-to-all-start.2 = ((f32[64,1,256]{2,1,0:T(1,128)}), f32[64,1,256]{2,1,0:T(1,128)S(1)}, u32[]{:S(2)}, u32[]{:S(2)}) async-start(f32[64,1,256]{2,1,0:T(1,128)} %reshape.306), calls=%async_computation.2 | async-start | bytes 131072 | tf_op jit(solution)/shard_map/all_to_all | solution.py:63
  75.1 1.9 copy.52
  77.0 4.4 %gather_fusion = f32[1024,6]{1,0:T(8,128)S(1)} fusion(f32[6,4096]{0,1:T(8,128)} %bitcast.72, s32[1024]{0:T(1024)S(1)} %broadcast_clamp_fusion.2), kind=kCustom, calls=%fused_computation | custom fusion | bytes 53248 | tf_op jit(solution)/shard_map/gather | solution.py:84
  81.4 22.9 %scatter_fusion = f32[6,1024]{0,1:T(8,128)S(1)} fusion(f32[6,1024]{0,1:T(8,128)S(1)} %bitcast.70, s32[4096]{0:T(1024)} %bitcast.86, f32[4096,6]{1,0:T(8,128)} %copy.56), kind=kCustom, calls=%fused_computation.3 | custom fusion | flops 24576 | bytes 311296 | tf_op jit(solution)/shard_map/vmap()/scatter-add | solution.py:91
  104.3 1.9 bitcast_subtract_fusion.2
  106.2 1.2 copy.58
  107.4 1.0 multiply_reduce_fusion.1
  109.0 0.8 reduce.26
  110.0 2.0 copy.62
  112.0 22.9 %scatter_custom_fusion.1 = f32[4,512]{0,1:T(8,128)S(1)} fusion(s32[4096]{0:T(1024)} %reshape.232, f32[4096,4]{1,0:T(8,128)} %copy.62, f32[]{:T(128)} %constant.9.clone.1), kind=kCustom, calls=%fused_computation.22 | custom fusion | flops 16384 | bytes 8704 | tf_op jit(solution)/shard_map/vmap()/scatter-add | solution.py:67
  135.2 0.8 fusion.3
  136.1 14.1 %gather_fusion.2 = f32[4096,3]{1,0:T(8,128)} fusion(f32[3,512]{0,1:T(8,128)S(1)} %get-tuple-element.31, s32[4096]{0:T(1024)S(1)} %copy-done.6), kind=kCustom, calls=%fused_computation.2 | custom fusion | bytes 114688 | tf_op jit(solution)/shard_map/gather | solution.py:71
  150.1 2.3 copy.63
  152.4 0.8 reshape.308
  153.2 10.3 %all-to-all-start.3 = ((f32[64,1,192]{2,1,0:T(1,128)}), f32[64,1,192]{2,1,0:T(1,128)S(1)}, u32[]{:S(2)}, u32[]{:S(2)}) async-start(f32[64,1,192]{2,1,0:T(1,128)} %reshape.308), calls=%async_computation.3 | async-start | bytes 131072 | tf_op jit(solution)/shard_map/all_to_all | solution.py:72
  163.5 0.6 reshape_add_fusion
  164.1 0.7 copy.68
  165.5 0.7 dynamic-update-slice.4
  166.2 6.1 %all-to-all-done.3 = f32[64,1,192]{2,1,0:T(1,128)S(1)} async-done(((f32[64,1,192]{2,1,0:T(1,128)}), f32[64,1,192]{2,1,0:T(1,128)S(1)}, u32[]{:S(2)}, u32[]{:S(2)}) %all-to-all-start.3) | async-done | bytes 49184 | tf_op jit(solution)/shard_map/all_to_all | solution.py:72
  172.3 0.8 reduce.27
  173.2 2.0 copy.67
  175.3 2.5 %fusion.2 = f32[]{:T(128)} fusion(f32[3,64,64]{0,2,1:T(8,128)} %copy.67, f32[4096]{0:T(1024)S(1)} %copy-done.5, f32[1,1,3,4096]{2,3,1,0:T(8,128)S(1)} %copy.54), kind=kLoop, calls=%fused_computation.8 | loop fusion | flops 49151 | bytes 114692 | tf_op jit(solution)/shard_map/reduce_sum | solution.py:75
  177.8 1.4 dynamic-update-slice
  179.2 9.1 %all-reduce.10 = (f32[4]{0:T(128)S(1)}, f32[4]{0:T(128)S(1)}) all-reduce(f32[4]{0:T(128)S(1)} %dynamic-update-slice.4, f32[4]{0:T(128)S(1)} %dynamic-update-slice), channel_id=1, replica_groups=mesh['robot_0'=4,'robot_1'=8,'robot_2'=2,'sub'=4] {'robot_0'}, use_global_device_ids=true, to_apply=%add.4 | all-reduce | flops 8 | bytes 64
  189.5 1.3 dynamic-update-slice.1
  190.8 1.3 dynamic-update-slice.5
  192.2 14.9 %all-reduce.8 = (f32[8]{0:T(128)S(1)}, f32[8]{0:T(128)S(1)}) all-reduce(f32[8]{0:T(128)S(1)} %dynamic-update-slice.5, f32[8]{0:T(128)S(1)} %dynamic-update-slice.1), channel_id=1, replica_groups=mesh['robot_0'=4,'robot_1'=8,'robot_2'=2,'sub'=4] {'robot_1'}, use_global_device_ids=true, to_apply=%add.5 | all-reduce | flops 16 | bytes 128
  208.3 1.3 dynamic-update-slice.2
  209.6 1.3 dynamic-update-slice.6
  211.0 2.5 %all-reduce.11 = (f32[2]{0:T(128)S(1)}, f32[2]{0:T(128)S(1)}) all-reduce(f32[2]{0:T(128)S(1)} %dynamic-update-slice.6, f32[2]{0:T(128)S(1)} %dynamic-update-slice.2), channel_id=1, replica_groups=mesh['robot_0'=4,'robot_1'=8,'robot_2'=2,'sub'=4] {'robot_2'}, use_global_device_ids=true, to_apply=%add.6 | all-reduce | flops 4 | bytes 32
  214.7 1.4 dynamic-update-slice.3
  216.2 1.4 dynamic-update-slice.7
  217.6 0.7 copy.69
  218.3 8.9 %all-reduce.9 = (f32[4]{0:T(128)S(1)}, f32[4]{0:T(128)S(1)}) all-reduce(f32[4]{0:T(128)S(1)} %dynamic-update-slice.7, f32[4]{0:T(128)S(1)} %dynamic-update-slice.3), channel_id=1, replica_groups=mesh['robot_0'=4,'robot_1'=8,'robot_2'=2,'sub'=4] {'sub'}, use_global_device_ids=true, to_apply=%add.7 | all-reduce | flops 8 | bytes 64
  227.7 0.7 reduce_sum.122
  228.4 1.8 fusion.10
  (66 shorter events, 7.0 us)
Async XLA Ops:
  0.6 17.6 %copy-start = (f32[1,1,3,4096]{3,1,2,0:T(1,128)S(1)}, f32[1,1,3,4096]{3,1,2,0:T(1,128)}, u32[]{:S(2)}) copy-start(f32[1,1,3,4096]{3,1,2,0:T(1,128)} %param.13) | copy-start | bytes 147460
  0.6 17.6 %copy-start.3 = (f32[1,1,3,4096]{3,1,2,0:T(1,128)S(1)}, f32[1,1,3,4096]{3,1,2,0:T(1,128)}, u32[]{:S(2)}) copy-start(f32[1,1,3,4096]{3,1,2,0:T(1,128)} %param.14) | copy-start | bytes 147460
  0.7 17.9 %copy-start.9 = (s32[1,1,4096]{2,1,0:T(1,128)S(1)}, s32[1,1,4096]{2,1,0:T(1,128)}, u32[]{:S(2)}) copy-start(s32[1,1,4096]{2,1,0:T(1,128)} %param.23) | copy-start | bytes 49156
  0.7 17.9 %copy-start.7 = (f32[1,1,3,4096]{3,1,2,0:T(1,128)S(1)}, f32[1,1,3,4096]{3,1,2,0:T(1,128)}, u32[]{:S(2)}) copy-start(f32[1,1,3,4096]{3,1,2,0:T(1,128)} %param.21) | copy-start | bytes 147460
  3.3 50.3 %all-to-all-start.1 = ((s32[1,64,64]{2,0,1:T(1,128)}), s32[1,64,64]{2,0,1:T(1,128)S(1)}, u32[]{:S(2)}, u32[]{:S(2)}) async-start(s32[1,64,64]{2,0,1:T(1,128)} %all_to_all.26), calls=%async_computation.1 | async-start | bytes 65536 | tf_op jit(solution)/shard_map/all_to_all | solution.py:64
  38.4 2.3 copy-start.1
  38.4 3.0 %copy-start.10 = (s32[1,1,1024]{2,1,0:T(1,128)S(1)}, s32[1,1,1024]{2,1,0:T(1,128)}, u32[]{:S(2)}) copy-start(s32[1,1,1024]{2,1,0:T(1,128)} %param.24) | copy-start | bytes 12292
  38.4 3.9 %copy-start.2 = (f32[1,1,6,1024]{3,1,2,0:T(1,128)S(1)}, f32[1,1,6,1024]{3,1,2,0:T(1,128)}, u32[]{:S(2)}) copy-start(f32[1,1,6,1024]{3,1,2,0:T(1,128)} %param.18) | copy-start | bytes 73732
  40.6 7.4 %copy-start.11 = (u32[256]{0:T(256)S(1)}, u32[256]{0:T(256)}, u32[]{:S(2)}) copy-start(u32[256]{0:T(256)} %constant.49) | copy-start | bytes 3076
  41.5 9.1 %copy-start.8 = (f32[1,1,6,1024]{3,1,2,0:T(1,128)S(1)}, f32[1,1,6,1024]{3,1,2,0:T(1,128)}, u32[]{:S(2)}) copy-start(f32[1,1,6,1024]{3,1,2,0:T(1,128)} %param.25) | copy-start | bytes 73732
  54.3 10.4 %all-to-all-start = ((f32[4,6,1024]{2,1,0:T(8,128)}), f32[4,6,1024]{2,1,0:T(8,128)S(1)}, u32[]{:S(2)}, u32[]{:S(2)}) async-start(f32[4,6,1024]{2,1,0:T(8,128)} %broadcast_in_dim.9), calls=%async_computation | async-start | bytes 262144 | tf_op jit(solution)/shard_map/all_to_all | solution.py:20
  64.7 43.7 %all-to-all-start.2 = ((f32[64,1,256]{2,1,0:T(1,128)}), f32[64,1,256]{2,1,0:T(1,128)S(1)}, u32[]{:S(2)}, u32[]{:S(2)}) async-start(f32[64,1,256]{2,1,0:T(1,128)} %reshape.306), calls=%async_computation.2 | async-start | bytes 131072 | tf_op jit(solution)/shard_map/all_to_all | solution.py:63
  109.8 26.3 %copy-start.6 = (s32[4096]{0:T(1024)S(1)}, s32[4096]{0:T(1024)}, u32[]{:S(2)}) copy-start(s32[4096]{0:T(1024)} %broadcast_clamp_fusion) | copy-start | bytes 49156
  152.4 22.9 %copy-start.5 = (f32[4096]{0:T(1024)S(1)}, f32[4096]{0:T(1024)}, u32[]{:S(2)}) copy-start(f32[4096]{0:T(1024)} %reshape.197) | copy-start | bytes 49156
  153.2 19.1 %all-to-all-start.3 = ((f32[64,1,192]{2,1,0:T(1,128)}), f32[64,1,192]{2,1,0:T(1,128)S(1)}, u32[]{:S(2)}, u32[]{:S(2)}) async-start(f32[64,1,192]{2,1,0:T(1,128)} %reshape.308), calls=%async_computation.3 | async-start | bytes 131072 | tf_op jit(solution)/shard_map/all_to_all | solution.py:72
  175.3 35.7 %copy-start.4 = (f32[1,1,3,4096]{3,1,2,0:T(1,128)S(1)}, f32[1,1,3,4096]{3,1,2,0:T(1,128)}, u32[]{:S(2)}) copy-start(f32[1,1,3,4096]{3,1,2,0:T(1,128)} %param.14) | copy-start | bytes 147460
